TPU v7x, 32 devices: a whole 2x2x4 slice. The times are simulated.
32 devices in a mesh: row: 8 (over z, y), col: 4 (over x, core).
Axes of the slice: x: 2, y: 2, z: 4, core: 2. Of those that a mesh axis runs over, the one named last changes fastest.
Arguments:
- matrix: float32 [1536, 1536], P('row', 'col'), may hold values from -30 to 30
- panels: float32 [2, 1536, 256], P(None, ('col', 'row')), may hold values from -0.15625 to 0.15625
- factors: float32 [2, 256, 256], replicated, may hold values from -1 to 2, as said below
Outputs:
- reduced: float32 [1536, 1536], P('row', 'col')
Inputs may be any that keep to these rules, and one draw needn't show every extreme that they name: Each factors[s] is upper triangular with diagonal entries between 1 and 2.
All inputs are finite; a program needn't handle non-finite values.
Results may differ from a plain program's by a relative error of at most 0.0003.
Values sent between devices are 32-bit elements; how exact they have to be, the bound alone decides.
No kernel may reach another device: no remote copies, remote signals or barrier semaphores. Data moves between devices by JAX's collectives and lax.ppermute only.
A program may use at most 64 MiB of HBM per device.

v0:
```python
import jax
import jax.numpy as jnp
from jax import lax
from jax.sharding import PartitionSpec as P

highest = lax.Precision.HIGHEST


def from_root(block, axis, owner):
    block = jnp.where(lax.axis_index(axis) == owner, block, jnp.zeros_like(block))
    return lax.psum(block, axis)


def matmul(left, right):
    return jnp.dot(left, right, precision=highest, preferred_element_type=jnp.float32)


def transposed_product(left, right):
    return lax.dot_general(
        left, right, (((0,), (0,)), ((), ())), precision=highest, preferred_element_type=jnp.float32
    )


def outer_product(left, right):
    return lax.dot_general(
        left, right, (((1,), (1,)), ((), ())), precision=highest, preferred_element_type=jnp.float32
    )


def per_device(matrix, panels, factors):
    row_count = lax.axis_size("row")
    col_count = lax.axis_size("col")
    my_row = lax.axis_index("row")
    block_rows = matrix.shape[0]
    share = panels.shape[1]
    source = my_row * col_count // row_count
    offset = share * (my_row * col_count - source * row_count)
    gathered = lax.all_gather(panels, "row", axis=1, tiled=True)
    relayed = from_root(gathered, "col", source)
    current = matrix
    for section in range(panels.shape[0]):
        factor = factors[section]
        panel_cols = gathered[section]
        panel_rows = lax.dynamic_slice_in_dim(relayed[section], offset, block_rows, 0)
        sums_rows = lax.psum(matmul(current, panel_cols), "col")
        sums_cols = lax.psum(transposed_product(current, panel_rows), "row")
        image_rows = matmul(sums_rows, factor)
        image_cols = matmul(sums_cols, factor)
        inner = lax.psum(transposed_product(panel_rows, image_rows), "row")
        correction = transposed_product(factor, inner)
        update_rows = image_rows - 0.5 * matmul(panel_rows, correction)
        update_cols = image_cols - 0.5 * matmul(panel_cols, correction)
        current = (
            current
            - outer_product(panel_rows, update_cols)
            - outer_product(update_rows, panel_cols)
        )
    return current


def solution(mesh):
    return jax.shard_map(
        per_device,
        mesh=mesh,
        in_specs=(P("row", "col"), P(None, ("col", "row"), None), P()),
        out_specs=P("row", "col"),
        check_vma=False,
    )
```

profile of v0, /device:TPU:0, one launch (start us, length us, event | category | flops | bytes accessed | tf_op | source)
XLA Modules:
  0.0 285.3 jit_solution(409260807775912355)
XLA Ops:
  6.5 0.0 all-reduce.14.cloned.1.call-start
  6.5 0.0 copy-start.1
  6.5 34.2 %all_gather.3 = f32[2,384,256]{2,1,0:T(8,128)S(1)} all-gather(f32[2,48,256]{2,1,0:T(8,128)} %param.4), channel_id=1, replica_groups=mesh['row'=8,'col'=4] {'row'}, dimensions={1}, use_global_device_ids=true | all-gather | bytes 884736 | tf_op jit(solution)/shard_map/all_gather | solution.py:38
  40.8 0.0 copy-done.1
  40.8 1.2 fusion.4
  41.9 1.0 broadcast_select_fusion
  42.9 0.0 all-reduce.14.cloned.1.call-update
  42.9 0.0 all-reduce.12.cloned.1.call-start
  43.0 36.9 %all-reduce.14.cloned.1.call-done = (f32[192,256]{1,0:T(8,128)}, f32[2,384,256]{2,1,0:T(8,128)}) async-done(((f32[192,256]{1,0:T(8,128)}, f32[2,384,256]{2,1,0:T(8,128)}), (f32[192,256]{1,0:T(8,128)}, f32[2,384,256]{2,1,0:T(8,128)})) %all-reduce.14.cloned.1.call-update) | async-done | bytes 983056 | tf_op jit(solution)/shard_map/psum | solution.py:45
  79.9 0.0 copy-start
  79.9 0.0 copy-start.4
  79.9 1.2 fusion.49
  81.1 0.0 copy-done
  81.1 0.0 copy-done.4
  81.2 0.3 fusion.13
  81.5 1.4 convolution_bitcast_fusion
  82.9 1.4 fusion.30
  84.3 0.0 all-reduce.12.cloned.1.call-update
  84.3 0.0 all-reduce.8.cloned.1.call-start
  84.4 74.2 %all-reduce.12.cloned.1.call-done = (f32[256,256]{1,0:T(8,128)}, f32[384,256]{0,1:T(8,128)}) async-done(((f32[256,256]{1,0:T(8,128)}, f32[384,256]{0,1:T(8,128)}), (f32[256,256]{1,0:T(8,128)}, f32[384,256]{0,1:T(8,128)})) %all-reduce.12.cloned.1.call-update) | async-done | bytes 655376 | tf_op jit(solution)/shard_map/psum | solution.py:49
  158.6 1.5 fusion.11
  160.2 0.4 fusion.3
  160.6 0.0 copy-start.2
  160.6 0.5 fusion.1
  161.1 0.5 copy-done.2
  161.6 0.8 convolution_subtract_fusion.1
  162.4 0.5 convolution_subtract_fusion.5
  162.9 0.5 convolution_subtract_fusion.4
  163.5 1.2 fusion.5
  164.7 0.0 all-reduce.8.cloned.1.call-update
  164.7 0.0 all-reduce.10.cloned.1.call-start
  164.7 1.6 fusion.26
  166.3 30.0 %all-reduce.8.cloned.1.call-done = f32[192,256]{1,0:T(8,128)} async-done(((f32[192,256]{1,0:T(8,128)}), f32[192,256]{1,0:T(8,128)}) %all-reduce.8.cloned.1.call-update) | async-done | bytes 196624 | tf_op jit(solution)/shard_map/psum | solution.py:45
  196.4 1.3 fusion.8
  197.6 1.4 fusion.24
  199.0 0.0 all-reduce.10.cloned.1.call-update
  199.0 74.5 %all-reduce.10.cloned.1.call-done = (f32[256,256]{1,0:T(8,128)}, f32[384,256]{1,0:T(8,128)}) async-done(((f32[256,256]{1,0:T(8,128)}, f32[384,256]{1,0:T(8,128)}), (f32[256,256]{1,0:T(8,128)}, f32[384,256]{1,0:T(8,128)})) %all-reduce.10.cloned.1.call-update) | async-done | bytes 655376 | tf_op jit(solution)/shard_map/psum | solution.py:49
  273.5 1.5 fusion.6
  275.1 0.4 fusion.2
  275.5 0.0 copy-start.3
  275.5 0.5 fusion
  276.0 0.5 copy-done.3
  276.5 0.5 convolution_subtract_fusion
  277.0 0.5 convolution_subtract_fusion.3
  277.5 1.3 convolution_subtract_fusion.2
Async XLA Ops:
  6.5 73.3 %all-reduce.14.cloned.1.call-start = ((), (), s32[]{:S(2)}) async-start(), calls=%async_computation.3 | async-start | bytes 1966080 | tf_op jit(solution)/shard_map/psum | solution.py:45
  6.5 34.2 %copy-start.1 = (f32[192,384]{1,0:T(8,128)S(1)}, f32[192,384]{1,0:T(8,128)}, u32[]{:S(2)}) copy-start(f32[192,384]{1,0:T(8,128)} %param.3) | copy-start | bytes 884740
  42.9 115.7 %all-reduce.12.cloned.1.call-start = ((), (), s32[]{:S(2)}) async-start(), calls=%async_computation.2 | async-start | bytes 1310720 | tf_op jit(solution)/shard_map/psum | solution.py:49
  79.9 1.3 copy-start
  79.9 1.3 copy-start.4
  84.3 112.0 %all-reduce.8.cloned.1.call-start = ((), (), s32[]{:S(2)}) async-start(), calls=%async_computation | async-start | bytes 393216 | tf_op jit(solution)/shard_map/psum | solution.py:45
  160.6 1.0 copy-start.2
  164.7 108.8 %all-reduce.10.cloned.1.call-start = ((), (), s32[]{:S(2)}) async-start(), calls=%async_computation.1 | async-start | bytes 1310720 | tf_op jit(solution)/shard_map/psum | solution.py:49
  275.5 1.0 copy-start.3
Sparse Core Ops, SparseCore 0:
  43.0 36.7 all-reduce.13
  84.5 74.1 all-reduce.11
  164.8 31.5 all-reduce.7
  199.7 73.7 all-reduce.9
where the time goes:
time: 286 us; the launch traced here: 285 us
  waiting for transfers between devices  216 us (76%)
  blocking collectives  34.2 us (12%)
  matrix products  18.8 us (7%)
  between operations  13.3 us (5%)
    psum x2, waiting for transfers between devices, per_device(): inner = lax.psum(transposed_product(panel_rows, image_rows), 'row')  149 us
    psum x2, waiting for transfers between devices, per_device(): sums_rows = lax.psum(matmul(current, panel_cols), 'col')  66.9 us
    all_gather x1, blocking collectives, per_device(): gathered = lax.all_gather(panels, 'row', axis=1, tiled=True)  34.2 us
    dot_general x6, matrix products, transposed_product(): lax.dot_general(left, right, (((0,), (0,)), ((), ())), precision=highest,...  8.86 us
    dot_general x10, matrix products, matmul(): jnp.dot(left, right, precision=highest, preferred_element_type=jnp.float32)  7.09 us
  transfers between devices with their start and end apart: 4, of which 4 were waited for; matrix products, arithmetic and copies ran while one was open for 1% of the time, Pallas kernels for 0%

commit v1 on v0

--- a/solution.py
+++ b/solution.py
@@ -42,7 +42,9 @@
         factor = factors[section]
         panel_cols = gathered[section]
         panel_rows = lax.dynamic_slice_in_dim(relayed[section], offset, block_rows, 0)
-        sums_rows = lax.psum(matmul(current, panel_cols), "col")
+        part = matmul(current, panel_cols)
+        blocks = lax.all_gather(part, "col", axis=0, tiled=False)
+        sums_rows = blocks.sum(axis=0)
         sums_cols = lax.psum(transposed_product(current, panel_rows), "row")
         image_rows = matmul(sums_rows, factor)
         image_cols = matmul(sums_cols, factor)

time: 286 us -> 258 us (0.902)
  waiting for transfers between devices: 216 us -> 170 us
  blocking collectives: 34.2 us -> 52.6 us
    psum x2 -> x1, waiting for transfers between devices: 66.9 us -> 23.9 us  [from_root(): return lax.psum(block, axis)]
    all_gather x0 -> x2, blocking collectives: none -> 18.5 us  [per_device(): blocks = lax.all_gather(part, 'col', axis=0, tiled=False)]
  transfers between devices with their start and end apart: 4 -> 3, of which waited for: 4 -> 3; matrix products, arithmetic and copies ran while one was open for 1% -> 0% of each run, Pallas kernels for 0% -> 0%
where the time goes in v1:
time: 258 us
  waiting for transfers between devices  170 us (66%)
  blocking collectives  52.6 us (20%)
  matrix products  16.5 us (6%)
  between operations  13.3 us (5%)
  local copies, waits for them, and re-layouts  3.97 us (2%)
    psum x2, waiting for transfers between devices, per_device(): inner = lax.psum(transposed_product(panel_rows, image_rows), 'row')  146 us
    all_gather x1, blocking collectives, per_device(): gathered = lax.all_gather(panels, 'row', axis=1, tiled=True)  34.1 us
    psum x1, waiting for transfers between devices, from_root(): return lax.psum(block, axis)  23.9 us
    all_gather x2, blocking collectives, per_device(): blocks = lax.all_gather(part, 'col', axis=0, tiled=False)  18.5 us
    dot_general x6, matrix products, transposed_product(): lax.dot_general(left, right, (((0,), (0,)), ((), ())), precision=highest,...  8.86 us
  transfers between devices with their start and end apart: 3, of which 3 were waited for; matrix products, arithmetic and copies ran while one was open for 0% of the time, Pallas kernels for 0%

profile of v1, /device:TPU:0, one launch (start us, length us, event | category | flops | bytes accessed | tf_op | source)
XLA Modules:
  0.0 257.9 jit_solution(14440347683205914332)
XLA Ops:
  6.5 0.0 all-reduce.6.cloned.1.call-start
  6.5 34.1 %all_gather.15 = f32[2,384,256]{2,1,0:T(8,128)S(1)} all-gather(f32[2,48,256]{2,1,0:T(8,128)} %param.4), channel_id=1, replica_groups=mesh['row'=8,'col'=4] {'row'}, dimensions={1}, use_global_device_ids=true | all-gather | bytes 884736 | tf_op jit(solution)/shard_map/all_gather | solution.py:38
  40.6 0.9 broadcast_select_fusion
  41.6 0.0 copy-start.1
  41.6 0.0 all-reduce.6.cloned.1.call-update
  41.6 0.0 all-reduce.10.cloned.1.call-start
  41.6 0.9 copy-done.1
  42.5 0.5 fusion.4
  43.0 9.9 %all-gather = f32[768,256]{1,0:T(8,128)S(1)} all-gather(f32[192,256]{1,0:T(8,128)S(1)} %fusion.4), channel_id=2, replica_groups=mesh['row'=8,'col'=4] {'col'}, dimensions={0}, use_global_device_ids=true | all-gather | bytes 983040 | tf_op jit(solution)/shard_map/all_gather | solution.py:46
  53.0 0.0 copy-start
  53.0 0.1 reduce_sum.18
  53.0 1.0 copy-done
  54.0 0.3 fusion.13
  54.3 23.9 %all-reduce.6.cloned.1.call-done = f32[2,384,256]{2,1,0:T(8,128)} async-done(((f32[2,384,256]{2,1,0:T(8,128)}), f32[2,384,256]{2,1,0:T(8,128)}) %all-reduce.6.cloned.1.call-update) | async-done | bytes 786448 | tf_op jit(solution)/shard_map/psum | solution.py:11
  78.3 1.2 fusion.49
  79.4 1.4 convolution_bitcast_fusion
  80.9 1.4 fusion.30
  82.2 0.0 all-reduce.10.cloned.1.call-update
  82.2 0.0 all-reduce.8.cloned.1.call-start
  82.3 73.9 %all-reduce.10.cloned.1.call-done = (f32[256,256]{1,0:T(8,128)}, f32[384,256]{0,1:T(8,128)}) async-done(((f32[256,256]{1,0:T(8,128)}, f32[384,256]{0,1:T(8,128)}), (f32[256,256]{1,0:T(8,128)}, f32[384,256]{0,1:T(8,128)})) %all-reduce.10.cloned.1.call-update) | async-done | bytes 655376 | tf_op jit(solution)/shard_map/psum | solution.py:51
  156.2 1.5 fusion.11
  157.7 0.4 fusion.3
  158.2 0.0 copy-start.2
  158.2 0.5 fusion.1
  158.7 0.5 copy-done.2
  159.2 0.8 convolution_subtract_fusion.1
  160.0 0.5 convolution_subtract_fusion.5
  160.5 0.5 convolution_subtract_fusion.4
  161.1 0.5 fusion.5
  161.6 1.6 fusion.26
  163.2 8.6 %all-gather.1 = f32[768,256]{1,0:T(8,128)S(1)} all-gather(f32[192,256]{1,0:T(8,128)S(1)} %fusion.5), channel_id=3, replica_groups=mesh['row'=8,'col'=4] {'col'}, dimensions={0}, use_global_device_ids=true | all-gather | bytes 983040 | tf_op jit(solution)/shard_map/all_gather | solution.py:46
  171.7 0.1 reduce_sum.19
  171.8 0.3 fusion.8
  172.1 1.4 fusion.24
  173.5 0.0 all-reduce.8.cloned.1.call-update
  173.5 72.6 %all-reduce.8.cloned.1.call-done = (f32[256,256]{1,0:T(8,128)}, f32[384,256]{1,0:T(8,128)}) async-done(((f32[256,256]{1,0:T(8,128)}, f32[384,256]{1,0:T(8,128)}), (f32[256,256]{1,0:T(8,128)}, f32[384,256]{1,0:T(8,128)})) %all-reduce.8.cloned.1.call-update) | async-done | bytes 655376 | tf_op jit(solution)/shard_map/psum | solution.py:51
  246.1 1.5 fusion.6
  247.6 0.4 fusion.2
  248.1 0.0 copy-start.3
  248.1 0.5 fusion
  248.6 0.5 copy-done.3
  249.1 0.5 convolution_subtract_fusion
  249.6 0.5 convolution_subtract_fusion.3
  250.1 1.3 convolution_subtract_fusion.2
Async XLA Ops:
  6.5 71.7 %all-reduce.6.cloned.1.call-start = ((), (), s32[]{:S(2)}) async-start(), calls=%async_computation | async-start | bytes 1572864 | tf_op jit(solution)/shard_map/psum | solution.py:11
  41.6 1.0 copy-start.1
  41.6 114.6 %all-reduce.10.cloned.1.call-start = ((), (), s32[]{:S(2)}) async-start(), calls=%async_computation.2 | async-start | bytes 1310720 | tf_op jit(solution)/shard_map/psum | solution.py:51
  53.0 1.0 copy-start
  82.2 163.8 %all-reduce.8.cloned.1.call-start = ((), (), s32[]{:S(2)}) async-start(), calls=%async_computation.1 | async-start | bytes 1310720 | tf_op jit(solution)/shard_map/psum | solution.py:51
  158.2 1.0 copy-start.2
  248.1 1.0 copy-start.3
Sparse Core Ops, SparseCore 0:
  41.7 36.5 all-reduce.5
  82.4 73.7 all-reduce.9
  173.7 72.3 all-reduce.7
